TPU v7x, 32 devices: a whole 2x2x4 slice. The times are simulated.
32 devices in a mesh: cell: 8 (over z, x), gene: 4 (over y, core).
Axes of the slice: x: 2, y: 2, z: 4, core: 2. Of those that a mesh axis runs over, the one named last changes fastest.
Arguments:
- counts: int32 [2048, 4096], P('cell', 'gene'), may hold values from 0 to 7
- totals: int32 [2048], P('cell'), may hold values from 1000 to 19999
- cell_factors: float32 [2048, 32], P('cell'), may hold values from -0.9 to 0.9
- gene_loadings: float32 [4096, 32], P('gene'), may hold values from -0.9 to 0.9
Outputs:
- new_factors: float32 [2048, 32], P('cell')
- new_loadings: float32 [4096, 32], P('gene')
- deviance: float32 [4096], P('gene')
All inputs are finite; a program needn't handle non-finite values.
Results may differ from a plain program's by a relative error of at most 0.0044.
Values sent between devices are 32-bit elements; how exact they have to be, the bound alone decides.
A program may use at most 128 MiB of HBM per device.

v0:
```python
import math

import jax
import jax.numpy as jnp
from jax import lax
from jax.sharding import PartitionSpec as P

RIDGE = 1.0
DAMPING = 0.1
SCALE_TOTAL = 5000.0


def outer_table(factors):
    width = factors.shape[1]
    product = factors[:, :, None] * factors[:, None, :]
    return product.reshape(factors.shape[0], width * width).astype(jnp.bfloat16)


def newton_solve(curvature, gradient):
    width = gradient.shape[1]
    matrix = jnp.transpose(curvature.reshape(gradient.shape[0], width, width), (1, 2, 0))
    diagonal_mean = sum((matrix[index, index] for index in range(width))) / width
    shift = RIDGE + DAMPING * diagonal_mean
    right = jnp.transpose(gradient)
    columns = []
    for column in range(width):
        current = matrix[:, column]
        if column > 0:
            stacked = jnp.stack(columns)
            current = current - jnp.sum(stacked * stacked[:, column][:, None, :], axis=0)
        current = (
            current
            + jnp.where(jnp.arange(width) == column, 1.0, 0.0).astype(jnp.float32)[:, None]
            * shift[None, :]
        )
        pivot = jnp.sqrt(current[column])
        mask = (jnp.arange(width) >= column).astype(jnp.float32)[:, None]
        columns.append(mask * current / pivot[None, :])
    lower = jnp.stack(columns, axis=1)
    forward = []
    for row in range(width):
        value = right[row]
        for inner in range(row):
            value = value - lower[row, inner] * forward[inner]
        forward.append(value / lower[row, row])
    backward = [None] * width
    for row in range(width - 1, -1, -1):
        value = forward[row]
        for inner in range(row + 1, width):
            value = value - lower[inner, row] * backward[inner]
        backward[row] = value / lower[row, row]
    return jnp.transpose(jnp.stack(backward))


def predict(offset, factors, loadings):
    linear = offset[:, None] + jnp.dot(factors, loadings.T, precision=lax.Precision.HIGHEST)
    return (linear, jnp.exp(linear))


def gene_contract(counts, expected, loadings, table_maker):
    weights = expected.astype(jnp.bfloat16)
    residual = (counts.astype(jnp.float32) - expected).astype(jnp.bfloat16)
    gradient = jnp.dot(residual, loadings.astype(jnp.bfloat16), preferred_element_type=jnp.float32)
    curvature = jnp.dot(weights, table_maker(loadings), preferred_element_type=jnp.float32)
    return (gradient, curvature)


def cell_contract(counts, linear, expected, factors, table_maker):
    counts_real = counts.astype(jnp.float32)
    weights = expected.astype(jnp.bfloat16)
    residual = (counts_real - expected).astype(jnp.bfloat16)
    dims = (((0,), (0,)), ((), ()))
    gradient = lax.dot_general(
        residual, factors.astype(jnp.bfloat16), dims, preferred_element_type=jnp.float32
    )
    curvature = lax.dot_general(
        weights, table_maker(factors), dims, preferred_element_type=jnp.float32
    )
    terms = 2.0 * (
        counts_real * (jnp.log(jnp.maximum(counts_real, 1.0)) - linear) - counts_real + expected
    )
    return (gradient, curvature, jnp.sum(terms, axis=0))


def on_device(counts, totals, cell_factors, gene_loadings):
    offset = jnp.log(totals.astype(jnp.float32)) - math.log(SCALE_TOTAL)
    linear, expected = predict(offset, cell_factors, gene_loadings)
    gradient_part, curvature_part = gene_contract(counts, expected, gene_loadings, outer_table)
    gradient_sum, curvature_sum = lax.psum((gradient_part, curvature_part), "gene")
    new_factors = cell_factors + newton_solve(curvature_sum, gradient_sum - RIDGE * cell_factors)
    cell_total = counts.shape[0] * lax.axis_size("cell")
    linear_next, expected_next = predict(offset, new_factors, gene_loadings)
    gradient_part, curvature_part, deviance_part = cell_contract(
        counts, linear_next, expected_next, new_factors, outer_table
    )
    gradient_share, curvature_share, deviance_share = (
        lax.psum_scatter(gradient_part, "cell", scatter_dimension=0, tiled=True),
        lax.psum_scatter(curvature_part, "cell", scatter_dimension=0, tiled=True),
        lax.psum_scatter(deviance_part, "cell", scatter_dimension=0, tiled=True),
    )
    portion = gradient_share.shape[0]
    start_row = lax.axis_index("cell") * portion
    own_rows = lax.dynamic_slice_in_dim(gene_loadings, start_row, portion, 0)
    own_new = own_rows + newton_solve(curvature_share, gradient_share - RIDGE * own_rows)
    new_loadings, deviance = (
        lax.all_gather(own_new, "cell", axis=0, tiled=True),
        lax.all_gather(deviance_share / cell_total, "cell", axis=0, tiled=True),
    )
    return (new_factors, new_loadings, deviance)


def solution(mesh):
    return jax.shard_map(
        on_device,
        mesh=mesh,
        in_specs=(P("cell", "gene"), P("cell"), P("cell", None), P("gene", None)),
        out_specs=(P("cell", None), P("gene", None), P("gene")),
        check_vma=False,
    )
```

profile of v0, /device:TPU:0, one launch (start us, length us, event | category | flops | bytes accessed | tf_op | source)
XLA Modules:
  0.0 289.5 jit_solution(2853326387708912902)
XLA Ops:
  7.2 0.7 log_add_fusion
  7.9 1.5 multiply_convert_fusion
  9.4 2.1 fusion
  11.6 0.8 fusion.7
  12.3 1.6 copy.132
  14.7 0.3 fusion.5
  15.0 13.8 %psum.14 = f32[256,32]{0,1:T(8,128)S(1)} all-reduce(f32[256,32]{0,1:T(8,128)S(1)} %fusion.5), channel_id=1, replica_groups=mesh['cell'=8,'gene'=4] {'gene'}, use_global_device_ids=true, to_apply=%region_0.0 | all-reduce | flops 8192 | bytes 65536 | tf_op jit(solution)/shard_map/psum | solution.py:89
  28.8 0.6 slice.8295
  29.4 23.9 %all-reduce.3.cloned.1.call-done = f32[32,32,256]{2,0,1:T(8,128)} async-done(((f32[32,32,256]{2,0,1:T(8,128)}), f32[32,32,256]{2,0,1:T(8,128)}) %all-reduce.3.cloned.1.call-update) | async-done | bytes 1048592 | tf_op jit(solution)/shard_map/psum | solution.py:89
  53.3 0.9 fusion.1423
  54.2 0.9 slice_add_fusion
  55.1 0.8 bitcast_add_fusion.2
  56.0 0.8 constant_dynamic-update-slice_fusion.454
  56.8 0.9 fusion.136
  57.8 0.9 constant_dynamic-update-slice_fusion.485
  58.7 0.8 fusion.134
  59.6 0.8 constant_dynamic-update-slice_fusion.452
  60.5 0.8 fusion.130
  61.4 0.8 constant_dynamic-update-slice_fusion.451
  62.4 0.8 fusion.126
  74.8 0.9 subtract_divide_fusion.12
  76.3 0.8 subtract_divide_fusion
  77.1 0.2 subtract_divide_fusion.92
  77.3 0.5 subtract_divide_fusion.81
  77.8 0.4 subtract_divide_fusion.74
  78.2 0.3 subtract_divide_fusion.57
  78.5 0.3 subtract_divide_fusion.48
  78.9 0.3 subtract_divide_fusion.42
  79.3 1.4 fusion.3
  80.9 0.9 fusion.6
  81.9 0.3 reduce-scatter.5.cloned.1.call-start
  82.2 2.7 fusion.4
  84.9 0.6 dynamic-slice
  86.2 21.4 %all-reduce = f32[1024]{0:T(1024)S(1)} all-reduce(f32[1024]{0:T(1024)S(1)} %get-tuple-element.1823), channel_id=4, replica_groups=mesh['cell'=8,'gene'=4] {'cell'}, use_global_device_ids=true, to_apply=%region_65.66.clone | all-reduce | flops 1024 | bytes 8192
  107.6 16.3 %all-gather = f32[8,1,128]{2,1,0:T(1,128)S(1)} all-gather(f32[1,1,128]{2,1,0:T(1,128)S(1)} %fusion.311), channel_id=1, replica_groups=mesh['cell'=8,'gene'=4] {'cell'}, dimensions={0}, use_global_device_ids=true | all-gather | bytes 4608 | tf_op jit(solution)/shard_map/all_gather | solution.py:107
  123.9 20.9 %reduce-scatter.3.cloned.1.call-done = f32[128,32]{0,1:T(8,128)} async-done(((f32[1024,32]{0,1:T(8,128)}), f32[128,32]{0,1:T(8,128)}) %reduce-scatter.3.cloned.1.call-update) | async-done | bytes 16400 | tf_op jit(solution)/shard_map/reduce_scatter | solution.py:97
  144.8 0.7 subtract_bitcast_fusion.1
  145.6 90.3 %reduce-scatter.5.cloned.1.call-done = f32[128,1024]{1,0:T(8,128)} async-done(((f32[1024,1024]{1,0:T(8,128)}), f32[128,1024]{1,0:T(8,128)}) %reduce-scatter.5.cloned.1.call-update) | async-done | bytes 524304 | tf_op jit(solution)/shard_map/reduce_scatter | solution.py:98
  235.8 1.2 copy.17
  237.1 0.3 copy.133
  248.0 0.3 subtract_divide_fusion.116
  248.3 0.4 bitcast_divide_fusion.1
  249.0 0.8 fusion.342
  249.8 0.5 fusion.1335
  250.3 0.8 subtract_divide_fusion.104
  251.2 30.5 %all_gather.6 = f32[1024,32]{0,1:T(8,128)S(1)} all-gather(f32[128,32]{0,1:T(8,128)S(1)} %bitcast_add_fusion.3), channel_id=1, replica_groups=mesh['cell'=8,'gene'=4] {'cell'}, dimensions={0}, use_global_device_ids=true | all-gather | bytes 147456 | tf_op jit(solution)/shard_map/all_gather | solution.py:106
  281.7 0.7 copy.1110
  282.4 0.6 copy.1111
  (634 shorter events, 22.0 us)
Async XLA Ops:
  7.2 46.1 %all-reduce.3.cloned.1.call-start = ((), (), s32[]{:S(2)}) async-start(), calls=%async_computation.2 | async-start | bytes 2097152 | tf_op jit(solution)/shard_map/psum | solution.py:89
  9.4 5.3 %copy-start.1 = (s32[256,1024]{1,0:T(8,128)S(1)}, s32[256,1024]{1,0:T(8,128)}, u32[]{:S(2)}) copy-start(s32[256,1024]{1,0:T(8,128)} %param.4) | copy-start | bytes 3145732
  9.4 5.3 %copy-start.2 = (f32[1024,32]{0,1:T(8,128)S(1)}, f32[1024,32]{0,1:T(8,128)}, u32[]{:S(2)}) copy-start(f32[1024,32]{0,1:T(8,128)} %param.7) | copy-start | bytes 393220
  11.5 17.2 %copy-start.4 = (f32[256,32]{0,1:T(8,128)S(1)}, f32[256,32]{0,1:T(8,128)}, u32[]{:S(2)}) copy-start(f32[256,32]{0,1:T(8,128)} %param.6) | copy-start | bytes 98308
  14.0 130.9 %reduce-scatter.3.cloned.1.call-start = ((), (), s32[]{:S(2)}) async-start(), calls=%async_computation.3 | async-start | bytes 147456 | tf_op jit(solution)/shard_map/reduce_scatter | solution.py:97
  53.3 10.1 %copy-start = (f32[32,32,256]{2,0,1:T(8,128)S(1)}, f32[32,32,256]{2,0,1:T(8,128)}, u32[]{:S(2)}) copy-start(f32[32,32,256]{2,0,1:T(8,128)} %all-reduce.3.cloned.1.call-done) | copy-start | bytes 3145732
  79.3 5.6 %copy-start.3 = (f32[256,32]{0,1:T(8,128)}, f32[256,32]{0,1:T(8,128)S(1)}, u32[]{:S(2)}) copy-start(f32[256,32]{0,1:T(8,128)S(1)} %bitcast_add_fusion) | copy-start | bytes 98308
  81.9 153.9 %reduce-scatter.5.cloned.1.call-start = ((), (), s32[]{:S(2)}) async-start(), calls=%async_computation.4 | async-start | bytes 4718592 | tf_op jit(solution)/shard_map/reduce_scatter | solution.py:98
  82.1 2.8 copy-start.5
Sparse Core Ops, SparseCore 0:
  14.1 39.1 all-reduce.2
  82.0 62.7 reduce-scatter.2
  148.5 87.3 reduce-scatter.4
where the time goes:
time: 291 us; the launch traced here: 290 us
  waiting for transfers between devices  135 us (46%)
  blocking collectives  81.9 us (28%)
  other arithmetic  35.1 us (12%)
  between operations  17.4 us (6%)
  local copies, waits for them, and re-layouts  11.5 us (4%)
  matrix products  8.22 us (3%)
    reduce_scatter x1, waiting for transfers between devices, on_device(): lax.psum_scatter(curvature_part, 'cell', scatter_dimension=0, tiled=True)  90.3 us
    all_gather x1, blocking collectives, on_device(): lax.all_gather(own_new, 'cell', axis=0, tiled=True)  30.5 us
    psum x1, waiting for transfers between devices, on_device(): lax.psum((gradient_part, curvature_part), 'gene')  23.9 us
    unnamed x1, blocking collectives  21.4 us
    reduce_scatter x1, waiting for transfers between devices, on_device(): lax.psum_scatter(gradient_part, 'cell', scatter_dimension=0, tiled=True)  20.9 us
    all_gather x1, blocking collectives, on_device(): lax.all_gather(deviance_share / cell_total, 'cell', axis=0, tiled=True)  16.3 us
    psum x1, blocking collectives, on_device(): lax.psum((gradient_part, curvature_part), 'gene')  13.8 us
    add x64, other arithmetic, newton_solve(): current + jnp.where(jnp.arange(width) == column, 1.0, 0.0).astype(jnp.flo...  8.72 us
  transfers between devices with their start and end apart: 3, of which 3 were waited for; matrix products, arithmetic and copies ran while one was open for 2% of the time, Pallas kernels for 0%

commit v1 on v0

v1 whole, which is shorter than its diff:
```python
import functools
import math

import jax
import jax.numpy as jnp
from jax import lax
from jax.experimental import pallas as pl
from jax.experimental.pallas import tpu as pltpu
from jax.sharding import PartitionSpec as P

RIDGE = 1.0
DAMPING = 0.1
SCALE_TOTAL = 5000.0
LANES = 128
SUB = 8
BLOCK = 256
HIGH = lax.Precision.HIGHEST
NT = (((1,), (1,)), ((), ()))
F32 = jnp.float32
BF16 = jnp.bfloat16


def packed_rows(width):
    return sum(width - SUB * (a // SUB) for a in range(width))


def lower_table(factors):
    width = factors.shape[0]
    pieces = [factors[a : a + 1] * factors[SUB * (a // SUB) :] for a in range(width)]
    return jnp.concatenate(pieces, axis=0).astype(BF16)


def solve_packed(get, right, width):
    blocks, start = [], 0
    for block in range(width // SUB):
        rows = width - SUB * block
        blocks.append(get(start, SUB * rows).reshape(SUB, rows, right.shape[1]))
        start += SUB * rows
    diagonal = sum(blocks[a // SUB][a % SUB, a % SUB : a % SUB + 1] for a in range(width)) / width
    shift = RIDGE + DAMPING * diagonal
    count = width // SUB
    index = lax.broadcasted_iota(jnp.int32, (width, right.shape[1]), 0)
    lower, scaled = [], []
    value = right
    for a in range(width):
        own, place = a // SUB, a % SUB
        column = blocks[own][place]
        rows = index[: width - SUB * own]
        inverse = 1.0 / (column[place : place + 1] + shift)
        factor = jnp.where(rows > place, column * inverse, 0.0)
        for block in range(own, count):
            offset = SUB * (block - own)
            coefficient = column[offset : offset + SUB]
            blocks[block] = blocks[block] - factor[offset:][None] * coefficient[:, None, :]
        lower.append(factor)
        head = value[SUB * own :]
        pivot = head[place : place + 1]
        scaled.append(pivot * inverse)
        head = head - factor * pivot
        value = head if own == 0 else jnp.concatenate([value[: SUB * own], head], axis=0)
    parts = [None] * count
    for a in range(width - 1, -1, -1):
        own, place = a // SUB, a % SUB
        rows = index[:SUB]
        if parts[own] is None:
            parts[own] = jnp.zeros((SUB, right.shape[1]), F32)
        known = jnp.concatenate(parts[own:], axis=0)
        found = scaled[a] - jnp.sum(lower[a] * known, axis=0, keepdims=True)
        parts[own] = jnp.where(rows == place, found, parts[own])
    return jnp.concatenate(parts, axis=0)


def solve_kernel(width, curvature_ref, gradient_ref, out_ref):
    out_ref[...] = solve_packed(
        lambda start, rows: curvature_ref[start : start + rows], gradient_ref[...], width
    )


def newton_solve(curvature, gradient):
    count, width = gradient.shape
    matrix = jnp.transpose(curvature).reshape(width, width, count)
    packed = jnp.concatenate([matrix[a, SUB * (a // SUB) :] for a in range(width)], axis=0)
    fill = -count % LANES
    packed = jnp.pad(packed, ((0, 0), (0, fill)))
    right = jnp.pad(jnp.transpose(gradient), ((0, 0), (0, fill)))
    rows = packed.shape[0]
    result = pl.pallas_call(
        functools.partial(solve_kernel, width),
        grid=((count + fill) // LANES,),
        in_specs=[
            pl.BlockSpec((rows, LANES), lambda i: (0, i)),
            pl.BlockSpec((width, LANES), lambda i: (0, i)),
        ],
        out_specs=pl.BlockSpec((width, LANES), lambda i: (0, i)),
        out_shape=jax.ShapeDtypeStruct(right.shape, F32),
    )(packed, right)
    return jnp.transpose(result[:, :count])


def outer_table(factors):
    width = factors.shape[1]
    product = factors[:, :, None] * factors[:, None, :]
    return product.reshape(factors.shape[0], width * width).astype(BF16)


def predict(offset, factors, loadings):
    linear = offset[:, None] + jnp.dot(factors, loadings.T, precision=HIGH)
    return (linear, jnp.exp(linear))


def gene_contract(counts, expected, loadings):
    weights = expected.astype(BF16)
    residual = (counts.astype(F32) - expected).astype(BF16)
    gradient = jnp.dot(residual, loadings.astype(BF16), preferred_element_type=F32)
    curvature = jnp.dot(weights, outer_table(loadings), preferred_element_type=F32)
    return (gradient, curvature)


def cell_contract(counts, linear, expected, factors):
    counts_real = counts.astype(F32)
    weights = expected.astype(BF16)
    residual = (counts_real - expected).astype(BF16)
    dims = (((0,), (0,)), ((), ()))
    gradient = lax.dot_general(residual, factors.astype(BF16), dims, preferred_element_type=F32)
    curvature = lax.dot_general(weights, outer_table(factors), dims, preferred_element_type=F32)
    terms = 2.0 * (
        counts_real * (jnp.log(jnp.maximum(counts_real, 1.0)) - linear) - counts_real + expected
    )
    return (gradient, curvature, jnp.sum(terms, axis=0))


def by_collectives(counts, totals, cell_factors, gene_loadings):
    offset = jnp.log(totals.astype(F32)) - math.log(SCALE_TOTAL)
    linear, expected = predict(offset, cell_factors, gene_loadings)
    gradient_part, curvature_part = gene_contract(counts, expected, gene_loadings)
    gradient_sum, curvature_sum = lax.psum((gradient_part, curvature_part), "gene")
    new_factors = cell_factors + newton_solve(curvature_sum, gradient_sum - RIDGE * cell_factors)
    cell_total = counts.shape[0] * lax.axis_size("cell")
    linear_next, expected_next = predict(offset, new_factors, gene_loadings)
    gradient_part, curvature_part, deviance_part = cell_contract(
        counts, linear_next, expected_next, new_factors
    )
    gradient_share, curvature_share, deviance_share = (
        lax.psum_scatter(gradient_part, "cell", scatter_dimension=0, tiled=True),
        lax.psum_scatter(curvature_part, "cell", scatter_dimension=0, tiled=True),
        lax.psum_scatter(deviance_part, "cell", scatter_dimension=0, tiled=True),
    )
    portion = gradient_share.shape[0]
    start_row = lax.axis_index("cell") * portion
    own_rows = lax.dynamic_slice_in_dim(gene_loadings, start_row, portion, 0)
    own_new = own_rows + newton_solve(curvature_share, gradient_share - RIDGE * own_rows)
    new_loadings, deviance = (
        lax.all_gather(own_new, "cell", axis=0, tiled=True),
        lax.all_gather(deviance_share / cell_total, "cell", axis=0, tiled=True),
    )
    return (new_factors, new_loadings, deviance)


def extended(rows, last):
    n = rows.shape[1]
    index = lax.broadcasted_iota(jnp.int32, (SUB, n), 0)
    return jnp.concatenate([rows, jnp.where(index == 0, last, 0.0)], axis=0)


def send(source, target, send_sem, recv_sem, device):
    return pltpu.make_async_remote_copy(
        src_ref=source,
        dst_ref=target,
        send_sem=send_sem,
        recv_sem=recv_sem,
        device_id=device,
        device_id_type=pl.DeviceIdType.MESH,
    )


def sweep_kernel(
    n_cell,
    n_gene,
    counts_ref,
    totals_ref,
    factors_ref,
    loadings_ref,
    new_factors_ref,
    new_loadings_ref,
    deviance_ref,
    all_counts,
    all_totals,
    total,
    share,
    arrived,
    own_factors,
    all_factors,
    sums,
    dev_sum,
    own_loadings,
    all_loadings,
    counts_out,
    counts_in,
    totals_out,
    totals_in,
    share_out,
    share_in,
    factors_out,
    factors_in,
    loadings_out,
    loadings_in,
):
    cell, gene = lax.axis_index("cell"), lax.axis_index("gene")
    cells, width = factors_ref.shape
    genes = loadings_ref.shape[0]
    devices = n_cell * n_gene
    half = LANES // 2
    me = cell * n_gene + gene

    def device(step):
        other = lax.rem(me + step, devices)
        return {"cell": other // n_gene, "gene": lax.rem(other, n_gene)}

    barrier = pltpu.get_barrier_semaphore()

    @pl.loop(1, devices)
    def _(step):
        pl.semaphore_signal(
            barrier, inc=1, device_id=device(step), device_id_type=pl.DeviceIdType.MESH
        )

    pl.semaphore_wait(barrier, devices - 1)

    early = []
    for step in range(1, n_cell):
        other = lax.rem(cell + step, n_cell)
        columns = pl.ds(pl.multiple_of(other * LANES, LANES), LANES)
        there = {"cell": other, "gene": gene}
        early.append(
            send(counts_ref.at[:, columns], all_counts.at[cell], counts_out.at[step], counts_in.at[step], there)
        )
        early.append(
            send(totals_ref, all_totals.at[cell], totals_out.at[step], totals_in.at[step], there)
        )
    for copy in early:
        copy.start()
    own_columns = pl.ds(pl.multiple_of(cell * LANES, LANES), LANES)
    all_counts[cell] = counts_ref[:, own_columns]
    all_totals[cell] = totals_ref[...]

    offset = jnp.log(totals_ref[...].astype(F32)) - math.log(SCALE_TOTAL)
    left = jnp.transpose(extended(jnp.transpose(factors_ref[...]), offset))
    total[...] = jnp.zeros_like(total)

    @pl.loop(0, genes // BLOCK)
    def _(block):
        where = pl.ds(pl.multiple_of(block * BLOCK, BLOCK), BLOCK)
        rows = jnp.transpose(loadings_ref[where, :])
        expected = jnp.exp(jnp.dot(left, extended(rows, 1.0), precision=HIGH, preferred_element_type=F32))
        weights = expected.astype(BF16)
        residual = (counts_ref[:, where].astype(F32) - expected).astype(BF16)
        total[:width] += lax.dot_general(rows.astype(BF16), residual, NT, preferred_element_type=F32)
        total[width:] += lax.dot_general(lower_table(rows), weights, NT, preferred_element_type=F32)

    size = total.shape[0] // 2
    lane = lax.broadcasted_iota(jnp.int32, (size, LANES), 1)
    for pair in range(n_gene // 2):
        columns = slice(pair * LANES, (pair + 1) * LANES)
        top, bottom = total[:size, columns], total[size:, columns]
        share[2 * pair] = jnp.where(lane < half, top, pltpu.roll(bottom, half, 1))
        share[2 * pair + 1] = jnp.where(lane < half, pltpu.roll(top, half, 1), bottom)
    shares = []
    for step in range(1, n_gene):
        other = lax.rem(gene + step, n_gene)
        there = {"cell": cell, "gene": other}
        shares.append(
            send(share.at[other], arrived.at[step], share_out.at[step], share_in.at[step], there)
        )
    for copy in shares:
        copy.start()
    own_rows = factors_ref[pl.ds(pl.multiple_of(gene * half, half), half), :]
    own_rows = jnp.transpose(jnp.concatenate([own_rows, own_rows], axis=0))
    for copy in shares:
        copy.wait()
    both = share[gene]
    for step in range(1, n_gene):
        both = both + arrived[step]
    sums[:size] = both
    sums[size:] = pltpu.roll(both, half, 1)
    found = own_rows + solve_packed(
        lambda start, rows: sums[width + start : width + start + rows],
        sums[:width] - RIDGE * own_rows,
        width,
    )
    lane = lax.broadcasted_iota(jnp.int32, (width // 2, LANES), 1)
    packed = jnp.where(lane < half, found[: width // 2], pltpu.roll(found[width // 2 :], half, 1))
    own_factors[...] = packed
    all_factors[me] = packed

    def factors_copy(step):
        return send(own_factors, all_factors.at[me], factors_out.at[step], factors_in.at[step], device(step))

    @pl.loop(1, devices)
    def _(step):
        factors_copy(step).start()

    own_genes = pl.ds(pl.multiple_of(cell * LANES, LANES), LANES)
    own_loadings_rows = jnp.transpose(loadings_ref[own_genes, :])
    right = extended(own_loadings_rows, 1.0)
    sums[...] = jnp.zeros_like(sums)
    dev_sum[...] = jnp.zeros_like(dev_sum)
    for copy in early:
        copy.wait()

    @pl.loop(1, devices)
    def _(step):
        factors_copy(step).wait()

    def cell_rows(index):
        tiles = []
        for pair in range(n_gene // 2):
            first = all_factors[index * n_gene + 2 * pair]
            second = all_factors[index * n_gene + 2 * pair + 1]
            top = jnp.where(lane < half, first, pltpu.roll(second, half, 1))
            bottom = jnp.where(lane < half, pltpu.roll(first, half, 1), second)
            tiles.append(jnp.concatenate([top, bottom], axis=0))
        return jnp.concatenate(tiles, axis=1)

    @pl.loop(0, n_cell)
    def _(index):
        rows = cell_rows(index)
        offsets = jnp.log(all_totals[index].astype(F32)) - math.log(SCALE_TOTAL)
        linear = jnp.dot(
            jnp.transpose(extended(rows, offsets)), right, precision=HIGH, preferred_element_type=F32
        )
        expected = jnp.exp(linear)
        real = all_counts[index].astype(F32)
        weights = expected.astype(BF16)
        residual = (real - expected).astype(BF16)
        sums[:width] += jnp.dot(rows.astype(BF16), residual, preferred_element_type=F32)
        sums[width:] += jnp.dot(lower_table(rows), weights, preferred_element_type=F32)
        terms = 2.0 * (real * (jnp.log(jnp.maximum(real, 1.0)) - linear) - real + expected)
        dev_sum[...] += jnp.sum(terms, axis=0, keepdims=True)

    new_rows = own_loadings_rows + solve_packed(
        lambda start, rows: sums[width + start : width + start + rows],
        sums[:width] - RIDGE * own_loadings_rows,
        width,
    )
    result = extended(new_rows, dev_sum[...] / (cells * n_cell))
    own_loadings[...] = result
    all_loadings[cell] = result
    last = []
    for step in range(1, n_cell):
        other = lax.rem(cell + step, n_cell)
        there = {"cell": other, "gene": gene}
        last.append(
            send(own_loadings, all_loadings.at[cell], loadings_out.at[step], loadings_in.at[step], there)
        )
    for copy in last:
        copy.start()
    new_factors_ref[...] = jnp.transpose(cell_rows(cell))
    for copy in last:
        copy.wait()
    for index in range(n_cell):
        block = all_loadings[index]
        new_loadings_ref[index * LANES : (index + 1) * LANES, :] = jnp.transpose(block[:width])
        deviance_ref[:, index * LANES : (index + 1) * LANES] = block[width : width + 1]


def by_kernel(n_cell, n_gene, counts, totals, cell_factors, gene_loadings):
    cells, genes = counts.shape
    width = cell_factors.shape[1]
    rows = width + packed_rows(width)
    devices = n_cell * n_gene
    vmem = pl.BlockSpec(memory_space=pltpu.VMEM)
    dma = lambda n: pltpu.SemaphoreType.DMA((n,))
    new_factors, new_loadings, deviance = pl.pallas_call(
        functools.partial(sweep_kernel, n_cell, n_gene),
        out_shape=(
            jax.ShapeDtypeStruct((cells, width), F32),
            jax.ShapeDtypeStruct((genes, width), F32),
            jax.ShapeDtypeStruct((1, genes), F32),
        ),
        in_specs=[vmem] * 4,
        out_specs=(vmem,) * 3,
        scratch_shapes=[
            pltpu.VMEM((n_cell, cells, LANES), jnp.int32),
            pltpu.VMEM((n_cell, 1, cells), jnp.int32),
            pltpu.VMEM((rows, cells), F32),
            pltpu.VMEM((n_gene, rows // 2, LANES), F32),
            pltpu.VMEM((n_gene, rows // 2, LANES), F32),
            pltpu.VMEM((width // 2, LANES), F32),
            pltpu.VMEM((devices, width // 2, LANES), F32),
            pltpu.VMEM((rows, LANES), F32),
            pltpu.VMEM((1, LANES), F32),
            pltpu.VMEM((width + SUB, LANES), F32),
            pltpu.VMEM((n_cell, width + SUB, LANES), F32),
            dma(n_cell),
            dma(n_cell),
            dma(n_cell),
            dma(n_cell),
            dma(n_gene),
            dma(n_gene),
            dma(devices),
            dma(devices),
            dma(n_cell),
            dma(n_cell),
        ],
        compiler_params=pltpu.CompilerParams(
            collective_id=0, has_side_effects=True, vmem_limit_bytes=48 * 1024 * 1024
        ),
    )(counts, totals.reshape(1, cells), cell_factors, gene_loadings)
    return (new_factors, new_loadings, deviance.reshape(genes))


def solution(mesh):
    n_cell, n_gene = mesh.shape["cell"], mesh.shape["gene"]

    def on_device(counts, totals, cell_factors, gene_loadings):
        cells, genes = counts.shape
        whole_lanes = genes == n_cell * LANES and 2 * cells == n_gene * LANES
        if whole_lanes and n_gene % 2 == 0 and genes % BLOCK == 0:
            return by_kernel(n_cell, n_gene, counts, totals, cell_factors, gene_loadings)
        return by_collectives(counts, totals, cell_factors, gene_loadings)

    return jax.shard_map(
        on_device,
        mesh=mesh,
        in_specs=(P("cell", "gene"), P("cell"), P("cell", None), P("gene", None)),
        out_specs=(P("cell", None), P("gene", None), P("gene")),
        check_vma=False,
    )
```

time: 291 us -> 56.4 us (0.19)
  waiting for transfers between devices: 135 us -> 0 us
  blocking collectives: 81.9 us -> 0 us
  Pallas kernels: 0 us -> 50.6 us
  other arithmetic: 35.1 us -> 0 us
  between operations: 17.4 us -> 0.66 us
  matrix products: 8.22 us -> 0 us
  local copies, waits for them, and re-layouts: 11.5 us -> 4.92 us
    reduce_scatter x2 -> x0, waiting for transfers between devices: 111 us -> none  [the longest x1 90.3 us: on_device(): lax.psum_scatter(curvature_part, 'cell', scatter_dimension=0, tiled=True)]
    pallas_call x0 -> x1, Pallas kernels: none -> 50.6 us  [by_kernel(): pl.pallas_call(functools.partial(sweep_kernel, n_cell, n_gene), out_shape...]
    all_gather x2 -> x0, blocking collectives: 46.8 us -> none  [the longest x1 30.5 us: on_device(): lax.all_gather(own_new, 'cell', axis=0, tiled=True)]
    psum x1 -> x0, waiting for transfers between devices: 23.9 us -> none  [on_device(): lax.psum((gradient_part, curvature_part), 'gene')]
    unnamed x1 -> x0, blocking collectives: 21.4 us -> none
    psum x1 -> x0, blocking collectives: 13.8 us -> none  [on_device(): lax.psum((gradient_part, curvature_part), 'gene')]
    div x72 -> x0, other arithmetic: 10.5 us -> none  [the longest x60 4.35 us: newton_solve(): columns.append(mask * current / pivot[None, :])]
    add x69 -> x0, other arithmetic: 9.7 us -> none  [the longest x64 8.72 us: newton_solve(): current + jnp.where(jnp.arange(width) == column, 1.0, 0.0).astype(jnp.flo...]
  transfers between devices with their start and end apart: 3 -> 0, of which waited for: 3 -> 0; matrix products, arithmetic and copies ran while one was open for 2% -> 0% of each run, Pallas kernels for 0% -> 0%
where the time goes in v1:
time: 56.4 us; the launch traced here: 56.2 us
  Pallas kernels  50.6 us (90%)
  local copies, waits for them, and re-layouts  4.92 us (9%)
  between operations  0.66 us (1%)
    pallas_call x1, Pallas kernels, by_kernel(): pl.pallas_call(functools.partial(sweep_kernel, n_cell, n_gene), out_shape...  50.6 us
    unnamed x11, local copies, waits for them, and re-layouts  4.92 us

profile of v1, /device:TPU:0, one launch (start us, length us, event | category | flops | bytes accessed | tf_op | source)
XLA Modules:
  0.0 56.2 jit_solution(15874630059640895638)
XLA Ops:
  0.6 0.0 copy-start.2
  0.6 0.9 %copy.7.factors_ref = f32[256,32]{1,0:T(8,128)S(1)} copy(f32[256,32]{0,1:T(8,128)} %param.6) | data formatting | bytes 65536 | tf_op args[2]
  1.5 0.0 copy-done.2
  1.6 0.0 copy-start.1
  1.6 0.2 copy.8.loadings_ref
  1.8 0.5 copy-done.1
  2.2 0.0 copy-start
  2.2 1.2 %copy-done = s32[256,1024]{1,0:T(8,128)S(1)} copy-done((s32[256,1024]{1,0:T(8,128)S(1)}, s32[256,1024]{1,0:T(8,128)}, u32[]{:S(2)}) %copy-start) | copy-done | bytes 1048600
  3.5 50.6 %shard_map.67 = (f32[256,32]{1,0:T(8,128)S(1)}, f32[1024,32]{1,0:T(8,128)S(1)}, f32[1,1024]{1,0:T(1,128)S(1)}) custom-call(s32[256,1024]{1,0:T(8,128)S(1)} %copy-done, s32[1,256]{1,0:T(1,128)S(1)} %bitcast.3, f32[256,32]{1,0:T(8,128)S(1)} %copy.7.factors_ref, f32[1024,32]{1,0:T(8,128)S(1)} %copy.8.loadings_ref), custom_call_target="tpu_custom_call" | custom-call | tf_op jit(solution)/shard_map/pallas_call | solution.py:373
  54.1 0.7 %copy.9 = f32[256,32]{0,1:T(8,128)} copy(f32[256,32]{1,0:T(8,128)S(1)} %get-tuple-element.9) | data formatting | bytes 65536
  54.8 0.8 %copy.10 = f32[1024,32]{0,1:T(8,128)} copy(f32[1024,32]{1,0:T(8,128)S(1)} %get-tuple-element.10) | data formatting | bytes 262144
  55.6 0.6 %copy.12 = f32[1024]{0:T(1024)} copy(f32[1024]{0:T(1024)S(1)} %bitcast.2) | data formatting | bytes 8192
Async XLA Ops:
  0.6 0.9 %copy-start.2 = (f32[1024,32]{0,1:T(8,128)S(1)}, f32[1024,32]{0,1:T(8,128)}, u32[]{:S(2)}) copy-start(f32[1024,32]{0,1:T(8,128)} %param.7) | copy-start | bytes 393220
  1.6 0.7 %copy-start.1 = (s32[256]{0:T(256)S(1)}, s32[256]{0:T(256)}, u32[]{:S(2)}) copy-start(s32[256]{0:T(256)} %param.5) | copy-start | bytes 3076
  2.2 1.2 %copy-start = (s32[256,1024]{1,0:T(8,128)S(1)}, s32[256,1024]{1,0:T(8,128)}, u32[]{:S(2)}) copy-start(s32[256,1024]{1,0:T(8,128)} %counts_ref.1) | copy-start | bytes 3145732

commit v2 on v1

--- a/solution.py
+++ b/solution.py
@@ -176,13 +176,14 @@
 def sweep_kernel(
     n_cell,
     n_gene,
-    counts_ref,
+    counts_hbm,
     totals_ref,
     factors_ref,
     loadings_ref,
     new_factors_ref,
     new_loadings_ref,
     deviance_ref,
+    counts_ref,
     all_counts,
     all_totals,
     total,
@@ -204,53 +205,66 @@
     factors_in,
     loadings_out,
     loadings_in,
+    local_sem,
 ):
     cell, gene = lax.axis_index("cell"), lax.axis_index("gene")
-    cells, width = factors_ref.shape
-    genes = loadings_ref.shape[0]
+    width, cells = factors_ref.shape
+    genes = loadings_ref.shape[1]
     devices = n_cell * n_gene
     half = LANES // 2
     me = cell * n_gene + gene
 
-    def device(step):
-        other = lax.rem(me + step, devices)
-        return {"cell": other // n_gene, "gene": lax.rem(other, n_gene)}
+    def device(cell_step, gene_step):
+        return {"cell": lax.rem(cell + cell_step, n_cell), "gene": lax.rem(gene + gene_step, n_gene)}
+
+    local = pltpu.make_async_copy(counts_hbm, counts_ref, local_sem)
+    local.start()
 
     barrier = pltpu.get_barrier_semaphore()
 
     @pl.loop(1, devices)
     def _(step):
         pl.semaphore_signal(
-            barrier, inc=1, device_id=device(step), device_id_type=pl.DeviceIdType.MESH
+            barrier, inc=1, device_id=device(step // n_gene, lax.rem(step, n_gene)), device_id_type=pl.DeviceIdType.MESH
         )
 
     pl.semaphore_wait(barrier, devices - 1)
 
-    early = []
-    for step in range(1, n_cell):
+    def counts_copy(step):
         other = lax.rem(cell + step, n_cell)
         columns = pl.ds(pl.multiple_of(other * LANES, LANES), LANES)
-        there = {"cell": other, "gene": gene}
-        early.append(
-            send(counts_ref.at[:, columns], all_counts.at[cell], counts_out.at[step], counts_in.at[step], there)
-        )
-        early.append(
-            send(totals_ref, all_totals.at[cell], totals_out.at[step], totals_in.at[step], there)
-        )
-    for copy in early:
-        copy.start()
+        return send(
+            counts_hbm.at[:, columns],
+            all_counts.at[cell],
+            counts_out.at[step],
+            counts_in.at[step],
+            device(step, 0),
+        )
+
+    def totals_copy(step):
+        return send(
+            totals_ref, all_totals.at[cell], totals_out.at[step], totals_in.at[step], device(step, 0)
+        )
+
+    near_first = []
+    for step in range(1, n_cell // 2 + 1):
+        near_first += [step] if 2 * step == n_cell else [step, n_cell - step]
+    for step in near_first[::-1]:
+        counts_copy(step).start()
+        totals_copy(step).start()
     own_columns = pl.ds(pl.multiple_of(cell * LANES, LANES), LANES)
+    all_totals[cell] = totals_ref[...]
+    local.wait()
     all_counts[cell] = counts_ref[:, own_columns]
-    all_totals[cell] = totals_ref[...]
 
     offset = jnp.log(totals_ref[...].astype(F32)) - math.log(SCALE_TOTAL)
-    left = jnp.transpose(extended(jnp.transpose(factors_ref[...]), offset))
+    left = jnp.transpose(extended(factors_ref[...], offset))
     total[...] = jnp.zeros_like(total)
 
     @pl.loop(0, genes // BLOCK)
     def _(block):
         where = pl.ds(pl.multiple_of(block * BLOCK, BLOCK), BLOCK)
-        rows = jnp.transpose(loadings_ref[where, :])
+        rows = loadings_ref[:, where]
         expected = jnp.exp(jnp.dot(left, extended(rows, 1.0), precision=HIGH, preferred_element_type=F32))
         weights = expected.astype(BF16)
         residual = (counts_ref[:, where].astype(F32) - expected).astype(BF16)
@@ -273,8 +287,8 @@
         )
     for copy in shares:
         copy.start()
-    own_rows = factors_ref[pl.ds(pl.multiple_of(gene * half, half), half), :]
-    own_rows = jnp.transpose(jnp.concatenate([own_rows, own_rows], axis=0))
+    pair_columns = pl.ds(pl.multiple_of(gene // 2 * LANES, LANES), LANES)
+    own_rows = pltpu.roll(factors_ref[:, pair_columns], half * lax.rem(gene, 2), 1)
     for copy in shares:
         copy.wait()
     both = share[gene]
@@ -292,24 +306,25 @@
     own_factors[...] = packed
     all_factors[me] = packed
 
-    def factors_copy(step):
-        return send(own_factors, all_factors.at[me], factors_out.at[step], factors_in.at[step], device(step))
-
-    @pl.loop(1, devices)
-    def _(step):
-        factors_copy(step).start()
-
-    own_genes = pl.ds(pl.multiple_of(cell * LANES, LANES), LANES)
-    own_loadings_rows = jnp.transpose(loadings_ref[own_genes, :])
+    def factors_copy(cell_step, gene_step):
+        index = cell_step * n_gene + gene_step
+        return send(
+            own_factors,
+            all_factors.at[me],
+            factors_out.at[index],
+            factors_in.at[index],
+            device(cell_step, gene_step),
+        )
+
+    for cell_step in near_first[::-1] + [0]:
+        for gene_step in range(n_gene):
+            if cell_step + gene_step:
+                factors_copy(cell_step, gene_step).start()
+
+    own_loadings_rows = loadings_ref[:, own_columns]
     right = extended(own_loadings_rows, 1.0)
     sums[...] = jnp.zeros_like(sums)
     dev_sum[...] = jnp.zeros_like(dev_sum)
-    for copy in early:
-        copy.wait()
-
-    @pl.loop(1, devices)
-    def _(step):
-        factors_copy(step).wait()
 
     def cell_rows(index):
         tiles = []
@@ -321,8 +336,7 @@
             tiles.append(jnp.concatenate([top, bottom], axis=0))
         return jnp.concatenate(tiles, axis=1)
 
-    @pl.loop(0, n_cell)
-    def _(index):
+    def add_cells(index):
         rows = cell_rows(index)
         offsets = jnp.log(all_totals[index].astype(F32)) - math.log(SCALE_TOTAL)
         linear = jnp.dot(
@@ -337,6 +351,21 @@
         terms = 2.0 * (real * (jnp.log(jnp.maximum(real, 1.0)) - linear) - real + expected)
         dev_sum[...] += jnp.sum(terms, axis=0, keepdims=True)
 
+    for gene_step in range(1, n_gene):
+        factors_copy(0, gene_step).wait()
+    new_factors_ref[...] = cell_rows(cell)
+    add_cells(cell)
+
+    @pl.loop(1, n_cell)
+    def _(place):
+        odd = lax.rem(place, 2)
+        step = odd * ((place + 1) // 2) + (1 - odd) * (n_cell - place // 2)
+        counts_copy(step).wait()
+        totals_copy(step).wait()
+        for gene_step in range(n_gene):
+            factors_copy(step, gene_step).wait()
+        add_cells(lax.rem(cell + n_cell - step, n_cell))
+
     new_rows = own_loadings_rows + solve_packed(
         lambda start, rows: sums[width + start : width + start + rows],
         sums[:width] - RIDGE * own_loadings_rows,
@@ -346,20 +375,18 @@
     own_loadings[...] = result
     all_loadings[cell] = result
     last = []
-    for step in range(1, n_cell):
-        other = lax.rem(cell + step, n_cell)
-        there = {"cell": other, "gene": gene}
+    for step in near_first[::-1]:
+        there = device(step, 0)
         last.append(
             send(own_loadings, all_loadings.at[cell], loadings_out.at[step], loadings_in.at[step], there)
         )
     for copy in last:
         copy.start()
-    new_factors_ref[...] = jnp.transpose(cell_rows(cell))
     for copy in last:
         copy.wait()
     for index in range(n_cell):
         block = all_loadings[index]
-        new_loadings_ref[index * LANES : (index + 1) * LANES, :] = jnp.transpose(block[:width])
+        new_loadings_ref[:, index * LANES : (index + 1) * LANES] = block[:width]
         deviance_ref[:, index * LANES : (index + 1) * LANES] = block[width : width + 1]
 
 
@@ -373,13 +400,14 @@
     new_factors, new_loadings, deviance = pl.pallas_call(
         functools.partial(sweep_kernel, n_cell, n_gene),
         out_shape=(
-            jax.ShapeDtypeStruct((cells, width), F32),
-            jax.ShapeDtypeStruct((genes, width), F32),
+            jax.ShapeDtypeStruct((width, cells), F32),
+            jax.ShapeDtypeStruct((width, genes), F32),
             jax.ShapeDtypeStruct((1, genes), F32),
         ),
-        in_specs=[vmem] * 4,
+        in_specs=[pl.BlockSpec(memory_space=pl.ANY)] + [vmem] * 3,
         out_specs=(vmem,) * 3,
         scratch_shapes=[
+            pltpu.VMEM((cells, genes), jnp.int32),
             pltpu.VMEM((n_cell, cells, LANES), jnp.int32),
             pltpu.VMEM((n_cell, 1, cells), jnp.int32),
             pltpu.VMEM((rows, cells), F32),
@@ -401,12 +429,13 @@
             dma(devices),
             dma(n_cell),
             dma(n_cell),
+            pltpu.SemaphoreType.DMA,
         ],
         compiler_params=pltpu.CompilerParams(
-            collective_id=0, has_side_effects=True, vmem_limit_bytes=48 * 1024 * 1024
+            collective_id=0, has_side_effects=True, vmem_limit_bytes=60 * 1024 * 1024
         ),
-    )(counts, totals.reshape(1, cells), cell_factors, gene_loadings)
-    return (new_factors, new_loadings, deviance.reshape(genes))
+    )(counts, totals.reshape(1, cells), cell_factors.T, gene_loadings.T)
+    return (new_factors.T, new_loadings.T, deviance.reshape(genes))
 
 
 def solution(mesh):

time: 56.4 us -> 54.4 us (0.965)
  local copies, waits for them, and re-layouts: 4.92 us -> 3.54 us
  Pallas kernels: 50.6 us -> 50 us
    unnamed x11 -> x5, local copies, waits for them, and re-layouts: 4.92 us -> 3.54 us
    pallas_call x1, Pallas kernels: 50.6 us -> 50 us  [by_kernel(): pl.pallas_call(functools.partial(sweep_kernel, n_cell, n_gene), out_shape...]
where the time goes in v2:
time: 54.4 us; the launch traced here: 54.2 us
  Pallas kernels  50 us (92%)
  local copies, waits for them, and re-layouts  3.54 us (7%)
  between operations  0.64 us (1%)
    pallas_call x1, Pallas kernels, by_kernel(): pl.pallas_call(functools.partial(sweep_kernel, n_cell, n_gene), out_shape...  50 us
    unnamed x5, local copies, waits for them, and re-layouts  3.54 us

profile of v2, /device:TPU:0, one launch (start us, length us, event | category | flops | bytes accessed | tf_op | source)
XLA Modules:
  0.0 54.2 jit_solution(9695461126668821247)
XLA Ops:
  0.6 50.0 %shard_map.67 = (f32[32,256]{1,0:T(8,128)}, f32[32,1024]{1,0:T(8,128)}, f32[1,1024]{1,0:T(1,128)}) custom-call(s32[256,1024]{1,0:T(8,128)} %counts_hbm.1, s32[1,256]{1,0:T(1,128)} %bitcast.11, f32[32,256]{1,0:T(8,128)} %bitcast.8, f32[32,1024]{1,0:T(8,128)} %bitcast.7), custom_call_target="tpu_custom_call" | custom-call | tf_op jit(solution)/shard_map/pallas_call | solution.py:400
  50.7 1.4 %copy.10 = f32[256,32]{0,1:T(8,128)} copy(f32[256,32]{0,1:T(8,128)} %bitcast.9) | data formatting | bytes 65536
  52.0 0.0 copy-start
  52.0 1.6 %copy.11 = f32[1024,32]{0,1:T(8,128)} copy(f32[1024,32]{0,1:T(8,128)} %bitcast.6) | data formatting | bytes 262144
  53.6 0.0 copy-done
  53.6 0.6 %copy.12 = f32[1024]{0:T(1024)} copy(f32[1024]{0:T(1024)S(1)} %bitcast.10) | data formatting | bytes 8192
Async XLA Ops:
  52.0 1.6 %copy-start = (f32[1,1024]{1,0:T(1,128)S(1)}, f32[1,1024]{1,0:T(1,128)}, u32[]{:S(2)}) copy-start(f32[1,1024]{1,0:T(1,128)} %get-tuple-element.8) | copy-start | bytes 12292
